TPU v7x, 128 devices: a whole 4x4x4 slice. The times are simulated.
128 devices in a mesh: gx: 16 (over x, z), gy: 8 (over y, core).
Axes of the slice: x: 4, y: 4, z: 4, core: 2. Of those that a mesh axis runs over, the one named last changes fastest.
Arguments:
- source_tiles: bfloat16 [384, 32, 192, 384], P(('gx', 'gy')), may hold values from -6 to 6
- tile_offsets: int32 [2, 384], P(None, ('gx', 'gy')), may hold values from -128 to 1920, as said below
- tile_shifts: int32 [384], P(('gx', 'gy')), may hold values from 0 to 63
- tile_counts: int32 [128], P(('gx', 'gy')), may hold values from 1 to 3, as said below
Outputs:
- merged_slab: float32 [32, 2048, 2048], P(None, 'gx', 'gy')
Inputs may be any that keep to these rules, and one draw needn't show every extreme that they name: `tile_offsets`: slot k belongs to the device of joined gx+gy index d = k // 3, that is gx index d // 8 and gy index d % 8. Its x offset lies from that gx index times 128 minus 64 up to that gx index times 128; its y offset from the gy index times 256 minus 128 up to the gy index times 256. So every tile covers its owner's whole block. `tile_counts`: entry d counts the used slots of device d; they are its first slots, the others are ignored. Both 1 and 3 occur in every draw.
All inputs are finite; a program needn't handle non-finite values.
Results may differ from a plain program's by a relative error of at most 0.0003.
Values sent between devices are 32-bit elements; how exact they have to be, the bound alone decides.
A program may use at most 192 MiB of HBM per device.

v0:
```python
import jax
import jax.numpy as jnp
from jax import lax
from jax.experimental import pallas as pl
from jax.experimental.pallas import tpu as pltpu
from jax.sharding import PartitionSpec as P

NZ = 32
BX = 128
BY = 256
TX = 192
TY = 384
CAP = 3
RAMP = 32
RX = 64
RY = 128
WX = BX + 2 * RX
WY = BY + 2 * RY
AHEAD = 3
BEHIND = 12
HOLD = 6
GROUP = 2
EDGE = 4
LOT = 4
LOTS = (NZ - EDGE) // LOT
CENTRE = (NZ - 2 * EDGE) // 2
ROWS = 16
BLOCKS = WY // 128
MESH = pl.DeviceIdType.MESH


def ramp(places, length):
    return jnp.minimum(jnp.minimum(places + 1, length - places), RAMP)


def taps(places, length, fraction):
    inside = (places >= 0) & (places < length)
    blend = jnp.where(inside, ramp(places, length), 0).astype(jnp.float32)
    last = jnp.where(places == length - 1, fraction, 0.0)
    return blend, blend * (1.0 - fraction + last), blend * fraction


def kernel(
    tiles, offsets_hbm, shifts_hbm, counts_hbm, out,
    source, low_rim, high_rim, low_mid, high_mid,
    from_low_rim, from_high_rim, from_low_mid, from_high_mid,
    left, right, from_left, from_right,
    even, odd, placed, spread_y, spread_x, inverse,
    ramps, ramps_from_low, ramps_from_high, around, around_left, around_right,
    offsets, shifts, counts, number_sem, load_sem, ramp_sem, send_sem, recv_rim, recv_mid, recv_side,
):
    gx = lax.axis_index("gx")
    gy = lax.axis_index("gy")
    has_low, has_high = gy > 0, gy < lax.axis_size("gy") - 1
    has_left, has_right = gx > 0, gx < lax.axis_size("gx") - 1
    below, above = {"gy": gy - 1}, {"gy": gy + 1}
    before, after = {"gx": gx - 1}, {"gx": gx + 1}

    def load(i):
        z = NZ - 1 - i
        return pltpu.make_async_copy(tiles.at[:, z], source.at[:, z], load_sem.at[i])

    def load_lot(lot):
        span = pl.ds(NZ - EDGE - LOT * (lot + 1), LOT)
        return pltpu.make_async_copy(
            tiles.at[:, span], source.at[:, span], load_sem.at[EDGE + lot]
        )

    def remote(src, dst, send, recv, place):
        return pltpu.make_async_remote_copy(
            src_ref=src, dst_ref=dst, send_sem=send, recv_sem=recv,
            device_id=place, device_id_type=MESH,
        )

    def rim(way, z, count):
        src, dst, place = (
            (low_rim, from_high_rim, below), (high_rim, from_low_rim, above)
        )[way]
        span = pl.ds(z, count)
        return remote(
            src.at[span], dst.at[span], send_sem.at[way], recv_rim.at[way, z], place
        )

    def middle(way, z, count):
        src, dst, place = (
            (low_mid, from_high_mid, below), (high_mid, from_low_mid, above)
        )[way]
        span = pl.ds(z, count)
        return remote(
            src.at[span], dst.at[span], send_sem.at[2 + way], recv_mid.at[way, z // GROUP], place
        )

    def side(way, z, count):
        src, dst, place = ((left, from_right, before), (right, from_left, after))[way]
        span = pl.ds(z, count)
        inner = jnp.minimum(jnp.maximum(z - EDGE, 0) // 2, CENTRE)
        last = jnp.maximum(z - NZ + EDGE, 0)
        at = jnp.minimum(z, EDGE) + inner + last
        return remote(
            src.at[span], dst.at[span], send_sem.at[4 + way], recv_side.at[way, at], place
        )

    def ramp_y(way):
        dst, place = ((ramps_from_high, below), (ramps_from_low, above))[way]
        return remote(ramps, dst, ramp_sem.at[way], ramp_sem.at[2 + way], place)

    def ramp_x(way):
        dst, place = ((around_right, before), (around_left, after))[way]
        return remote(around, dst, ramp_sem.at[4 + way], ramp_sem.at[6 + way], place)

    y_ways = ((0, has_low, has_high), (1, has_high, has_low))
    x_ways = ((0, has_left, has_right), (1, has_right, has_left))

    def start(ways, make, *place):
        for way, sends, _ in ways:
            @pl.when(sends)
            def _(way=way):
                make(way, *place).start()

    def sent(ways, make, *place):
        for way, sends, _ in ways:
            @pl.when(sends)
            def _(way=way):
                make(way, *place).wait_send()

    def arrived(ways, make, *place):
        for way, _, receives in ways:
            @pl.when(receives)
            def _(way=way):
                make(way, *place).wait_recv()

    numbers = [
        pltpu.make_async_copy(src, dst, number_sem.at[n])
        for n, (src, dst) in enumerate(
            ((offsets_hbm, offsets), (shifts_hbm, shifts), (counts_hbm, counts))
        )
    ]
    for copy in numbers:
        copy.start()
    for i in range(3):
        load(i).start()

    barrier = pltpu.get_barrier_semaphore()
    neighbours = (
        (has_low, below), (has_high, above), (has_left, before), (has_right, after)
    )
    for present, place in neighbours:
        @pl.when(present)
        def _(place=place):
            pl.semaphore_signal(barrier, inc=1, device_id=place, device_id_type=MESH)

    for copy in numbers:
        copy.wait()
    starts_x, starts_y, parts, used, tops = [], [], [], [], []
    for k in range(CAP):
        code = shifts[k]
        starts_x.append(offsets[0, k] - gx * BX + RX)
        starts_y.append(offsets[1, k] - gy * BY + RY)
        tops.append(jnp.minimum(jnp.maximum(RX - starts_x[k], 0), RX))
        parts.append([
            ((code >> bits) & 3).astype(jnp.float32) * 0.25 for bits in (4, 2, 0)
        ])
        used.append(jnp.where(k < counts[0], 1.0, 0.0).astype(jnp.float32))

    taps_y = [
        taps(lax.broadcasted_iota(jnp.int32, (8, WY), 1) - starts_y[k], TY, parts[k][2])
        for k in range(CAP)
    ]
    for k in range(CAP):
        for r in range(0, TY, 64):
            apart = (
                lax.broadcasted_iota(jnp.int32, (64, WY), 0) + r
                - lax.broadcasted_iota(jnp.int32, (64, WY), 1) + starts_y[k]
            )
            own, following = taps_y[k][1][0:1], taps_y[k][2][0:1]
            spread_y[k, r : r + 64] = jnp.where(
                apart == 0, own, jnp.where(apart == 1, following, 0.0)
            ).astype(jnp.bfloat16)

    for k in range(CAP):
        place = lax.broadcasted_iota(jnp.int32, (WX, 128), 0) - starts_x[k]
        _, own, following = taps(place, TX, parts[k][1])
        spread_x[k, 0] = own * used[k]
        spread_x[k, 1] = following * used[k]
    placed[:, :, :RX] = jnp.zeros((CAP, BLOCKS, RX, 128), jnp.float32)
    placed[:, :, RX + TX :] = jnp.zeros((CAP, BLOCKS, RX + 8, 128), jnp.float32)

    ramps[...] = jnp.zeros_like(ramps)
    for k in range(CAP):
        blend = taps(
            lax.broadcasted_iota(jnp.int32, (8, WX), 1) - starts_x[k], TX, parts[k][1]
        )[0]
        ramps[k : k + 1, :WX] = blend[0:1] * used[k]
        ramps[k : k + 1, WX:] = taps_y[k][0][0:1]

    def along_y(z, *volumes):
        for k in range(CAP):
            rows = jnp.dot(
                source[k, z], spread_y[k], preferred_element_type=jnp.float32
            )
            for volume in volumes:
                volume[k] = rows

    load(0).wait()
    along_y(NZ - 1, even, odd)

    load(3).start()
    for lot in range(LOTS):
        load_lot(lot).start()

    pl.semaphore_wait(
        barrier, sum(present.astype(jnp.int32) for present, _ in neighbours)
    )

    def along_z(now, then):
        for k in range(CAP):
            depth_part = parts[k][0]
            for r in range(0, TX, ROWS):
                volume = (1.0 - depth_part) * now[k, r : r + ROWS] + (
                    depth_part * then[k, r : r + ROWS]
                )
                for n in range(BLOCKS):
                    placed[k, n, RX + r : RX + r + ROWS] = volume[:, n * 128 : (n + 1) * 128]

    def along_x(i, rims):
        for r in range(0, WX, ROWS):
            in_rim = r < RX or r >= RX + BX
            rim_row = r if r < RX else r - BX
            weights = [
                (spread_x[k, 0, r : r + ROWS], spread_x[k, 1, r : r + ROWS])
                for k in range(CAP)
            ]
            for n in range(BLOCKS):
                at_end = n in (0, BLOCKS - 1)
                if rims != (in_rim and at_end):
                    continue
                total = None
                for k in range(CAP):
                    first = tops[k] + r
                    term = weights[k][0] * placed[k, n, pl.ds(first, ROWS)] + (
                        weights[k][1] * placed[k, n, pl.ds(first + 1, ROWS)]
                    )
                    total = term if total is None else total + term
                if rims:
                    (low_rim if n == 0 else high_rim)[i, rim_row : rim_row + ROWS] = total
                elif at_end:
                    (low_mid if n == 0 else high_mid)[i, r - RX : r - RX + ROWS] = total
                else:
                    lanes = slice((n - 1) * 128, n * 128)
                    if r < RX:
                        left[i, r : r + ROWS, lanes] = total
                    elif in_rim:
                        right[i, r - RX - BX : r - RX - BX + ROWS, lanes] = total
                    else:
                        out[NZ - 1 - i, r - RX : r - RX + ROWS, lanes] = total

    def gather_ramps():
        around[...] = jnp.zeros_like(around)
        around[0:8, :WX] = ramps[:, :WX]
        around[0:8, WX:] = ramps[:, WX + RY : WX + RY + BY]
        arrived(y_ways, ramp_y)

        @pl.when(has_low)
        def _():
            around[8:16, :WX] = ramps_from_low[:, :WX]
            around[8:16, WX : WX + RY] = ramps_from_low[:, WX + RY + BY :]

        @pl.when(has_high)
        def _():
            around[16:24, :WX] = ramps_from_high[:, :WX]
            around[16:24, WX + RY :] = ramps_from_high[:, WX : WX + RY]

        start(x_ways, ramp_x)

    def weights_of(rows):
        return lax.dot_general(
            rows[:, :WX].astype(jnp.bfloat16), rows[:, WX:].astype(jnp.bfloat16),
            (((0,), (0,)), ((), ())), preferred_element_type=jnp.float32,
        )

    def invert():
        inverse[...] = weights_of(around[...])[RX : RX + BX]
        arrived(x_ways, ramp_x)

        @pl.when(has_left)
        def _():
            inverse[:RX] += weights_of(around_left[...])[RX + BX :]

        @pl.when(has_right)
        def _():
            inverse[RX:] += weights_of(around_right[...])[:RX]

        inverse[...] = 1.0 / jnp.maximum(inverse[...], 1.0)

    def sides(z):
        @pl.when(has_low)
        def _():
            left[z, :, :RY] += from_low_rim[z, :RX]
            right[z, :, :RY] += from_low_rim[z, RX:]

        @pl.when(has_high)
        def _():
            left[z, :, RY:] += from_high_rim[z, :RX]
            right[z, :, RY:] += from_high_rim[z, RX:]

    def finish(i):
        z = NZ - 1 - i

        @pl.when(has_low)
        def _():
            out[z, :, :RY] += from_low_mid[i]

        @pl.when(has_high)
        def _():
            out[z, :, RY:] += from_high_mid[i]

        @pl.when(has_left)
        def _():
            out[z, :RX] += from_left[i]

        @pl.when(has_right)
        def _():
            out[z, RX:] += from_right[i]

        out[z] *= inverse[...]

    def alone(i):
        return (i < EDGE) | (i >= NZ - EDGE)

    def step(i, now, then):
        @pl.when(i < NZ)
        def _():
            z = NZ - 2 - i

            @pl.when(i + 1 < EDGE)
            def _():
                load(i + 1).wait()

            @pl.when((i + 1 >= EDGE) & (i + 1 < NZ) & ((i + 1) % LOT == 0))
            def _():
                load_lot((i + 1 - EDGE) // LOT).wait()

            along_z(now, then)
            along_y(jnp.maximum(z, 0), then)
            along_x(i, True)
            along_x(i, False)
            start(y_ways, rim, i, 1)

            @pl.when(i == 0)
            def _():
                start(y_ways, ramp_y)

            @pl.when((i % GROUP == GROUP - 1) & (i > HOLD))
            def _():
                start(y_ways, middle, i - HOLD - GROUP + 1, GROUP)

            @pl.when(i == NZ - 1)
            def _():
                for k in range(HOLD, 0, -GROUP):
                    start(y_ways, middle, NZ - k, GROUP)

        ready = i - AHEAD

        @pl.when((ready >= 0) & (ready < NZ))
        def _():
            arrived(y_ways, rim, ready, 1)
            sides(ready)

            @pl.when(alone(ready))
            def _():
                start(x_ways, side, ready, 1)

            @pl.when(jnp.logical_not(alone(ready)) & (ready % 2 == 1))
            def _():
                start(x_ways, side, ready - 1, 2)

            @pl.when(ready == 3)
            def _():
                gather_ramps()

        done = i - BEHIND

        @pl.when((done >= 0) & (done < NZ))
        def _():
            @pl.when(done == 0)
            def _():
                invert()

            @pl.when(done % GROUP == 0)
            def _():
                arrived(y_ways, middle, done, GROUP)

            @pl.when(alone(done))
            def _():
                arrived(x_ways, side, done, 1)

            @pl.when(jnp.logical_not(alone(done)) & (done % 2 == 0))
            def _():
                arrived(x_ways, side, done, 2)

            finish(done)

    def two_steps(pair, carry):
        step(2 * pair, even, odd)
        step(2 * pair + 1, odd, even)
        return carry

    lax.fori_loop(0, (NZ + BEHIND) // 2, two_steps, 0)

    sent(y_ways, ramp_y)
    sent(x_ways, ramp_x)

    sent(y_ways, rim, 0, NZ)
    sent(y_ways, middle, 0, NZ)
    sent(x_ways, side, 0, NZ)


def local(source_tiles, tile_offsets, tile_shifts, tile_counts):
    hbm = pl.BlockSpec(memory_space=pl.ANY)
    dma = pltpu.SemaphoreType.DMA
    volume = pltpu.VMEM((CAP, TX, WY), jnp.float32)
    halo = pltpu.VMEM((NZ, BX, RY), jnp.float32)
    flank = pltpu.VMEM((NZ, RX, BY), jnp.float32)
    ramps = pltpu.VMEM((8, WX + WY), jnp.float32)
    around = pltpu.VMEM((24, WX + BY), jnp.float32)
    return pl.pallas_call(
        kernel,
        out_shape=pltpu.VMEM((NZ, BX, BY), jnp.float32),
        in_specs=[hbm, hbm, hbm, hbm],
        out_specs=pl.BlockSpec(memory_space=pltpu.VMEM),
        scratch_shapes=[
            pltpu.VMEM((CAP, NZ, TX, TY), jnp.bfloat16),
            halo, halo, halo, halo, halo, halo, halo, halo,
            flank, flank, flank, flank,
            volume, volume,
            pltpu.VMEM((CAP, BLOCKS, RX + TX + RX + 8, 128), jnp.float32),
            pltpu.VMEM((CAP, TY, WY), jnp.bfloat16),
            pltpu.VMEM((CAP, 2, WX, 128), jnp.float32),
            pltpu.VMEM((BX, BY), jnp.float32),
            ramps, ramps, ramps, around, around, around,
            pltpu.SMEM((2, CAP), jnp.int32),
            pltpu.SMEM((CAP,), jnp.int32),
            pltpu.SMEM((1,), jnp.int32),
            dma((3,)), dma((EDGE + LOTS,)), dma((8,)),
            dma((6,)), dma((2, NZ)), dma((2, NZ // GROUP)), dma((2, 2 * EDGE + CENTRE)),
        ],
        compiler_params=pltpu.CompilerParams(
            collective_id=0, has_side_effects=True, vmem_limit_bytes=54 * 1024 * 1024,
        ),
    )(source_tiles, tile_offsets, tile_shifts, tile_counts)


def solution(mesh):
    placed = (
        P(("gx", "gy"), None, None, None),
        P(None, ("gx", "gy")),
        P(("gx", "gy")),
        P(("gx", "gy")),
    )
    return jax.shard_map(
        local, mesh=mesh, in_specs=placed, out_specs=P(None, "gx", "gy"), check_vma=False
    )
```

profile of v0, /device:TPU:15, one launch (start us, length us, event | category | flops | bytes accessed | tf_op | source)
XLA Modules:
  0.0 61.7 jit_solution(15966077040181671622)
XLA Ops:
  0.7 59.0 %shard_map.46 = f32[32,128,256]{2,1,0:T(8,128)S(1)} custom-call(bf16[3,32,192,384]{3,2,1,0:T(8,128)(2,1)} %tiles.1, s32[2,3]{1,0:T(2,128)} %offsets_hbm.1, s32[3]{0:T(128)} %shifts_hbm.1, s32[1]{0:T(128)S(6)} %copy.7.counts_hbm), custom_call_target="tpu_custom_call" | custom-call | tf_op jit(solution)/shard_map/pallas_call | solution.py:426
  59.7 2.0 %copy.6 = f32[32,128,256]{2,1,0:T(8,128)} copy(f32[32,128,256]{2,1,0:T(8,128)S(1)} %shard_map.46) | data formatting | bytes 8388608
where the time goes:
time: 61.9 us; the launch traced here: 61.7 us
  Pallas kernels  59 us (95%)
  local copies, waits for them, and re-layouts  2.02 us (3%)
  between operations  0.66 us (1%)
    pallas_call x1, Pallas kernels, local(): pl.pallas_call(kernel, out_shape=pltpu.VMEM((NZ, BX, BY), jnp.float32), i...  59 us
    unnamed x1, local copies, waits for them, and re-layouts  2.02 us

commit v1 on v0

--- a/solution.py
+++ b/solution.py
@@ -78,7 +78,7 @@
         )[way]
         span = pl.ds(z, count)
         return remote(
-            src.at[span], dst.at[span], send_sem.at[way], recv_rim.at[way, z], place
+            src.at[span], dst.at[span], send_sem.at[way], recv_rim.at[way, z % (2 * AHEAD + 2)], place
         )
 
     def middle(way, z, count):
@@ -442,7 +442,7 @@
             pltpu.SMEM((CAP,), jnp.int32),
             pltpu.SMEM((1,), jnp.int32),
             dma((3,)), dma((EDGE + LOTS,)), dma((8,)),
-            dma((6,)), dma((2, NZ)), dma((2, NZ // GROUP)), dma((2, 2 * EDGE + CENTRE)),
+            dma((6,)), dma((2, 2 * AHEAD + 2)), dma((2, NZ // GROUP)), dma((2, 2 * EDGE + CENTRE)),
         ],
         compiler_params=pltpu.CompilerParams(
             collective_id=0, has_side_effects=True, vmem_limit_bytes=54 * 1024 * 1024,

time: 61.9 us -> 61.3 us (level)
  no operation moved by 1% of the time
where the time goes in v1:
time: 61.3 us; the launch traced here: 61.2 us
  Pallas kernels  58.5 us (95%)
  local copies, waits for them, and re-layouts  2.02 us (3%)
  between operations  0.66 us (1%)
    pallas_call x1, Pallas kernels, local(): pl.pallas_call(kernel, out_shape=pltpu.VMEM((NZ, BX, BY), jnp.float32), i...  58.5 us
    unnamed x1, local copies, waits for them, and re-layouts  2.02 us

profile of v1, /device:TPU:15, one launch (start us, length us, event | category | flops | bytes accessed | tf_op | source)
XLA Modules:
  0.0 61.2 jit_solution(17933229948371139807)
XLA Ops:
  0.7 58.5 %shard_map.46 = f32[32,128,256]{2,1,0:T(8,128)S(1)} custom-call(bf16[3,32,192,384]{3,2,1,0:T(8,128)(2,1)} %tiles.1, s32[2,3]{1,0:T(2,128)} %offsets_hbm.1, s32[3]{0:T(128)} %shifts_hbm.1, s32[1]{0:T(128)S(6)} %copy.7.counts_hbm), custom_call_target="tpu_custom_call" | custom-call | tf_op jit(solution)/shard_map/pallas_call | solution.py:426
  59.2 2.0 %copy.6 = f32[32,128,256]{2,1,0:T(8,128)} copy(f32[32,128,256]{2,1,0:T(8,128)S(1)} %shard_map.46) | data formatting | bytes 8388608

commit v2 on v1

--- a/solution.py
+++ b/solution.py
@@ -17,9 +17,9 @@
 WX = BX + 2 * RX
 WY = BY + 2 * RY
 AHEAD = 3
-BEHIND = 12
-HOLD = 6
-GROUP = 2
+BEHIND = 14
+HOLD = 4
+GROUP = 4
 EDGE = 4
 LOT = 4
 LOTS = (NZ - EDGE) // LOT

time: 61.3 us -> 61.1 us (level)
  no operation moved by 1% of the time
where the time goes in v2:
time: 61.1 us; the launch traced here: 61 us
  Pallas kernels  58.3 us (95%)
  local copies, waits for them, and re-layouts  2.02 us (3%)
  between operations  0.66 us (1%)
    pallas_call x1, Pallas kernels, local(): pl.pallas_call(kernel, out_shape=pltpu.VMEM((NZ, BX, BY), jnp.float32), i...  58.3 us
    unnamed x1, local copies, waits for them, and re-layouts  2.02 us

profile of v2, /device:TPU:15, one launch (start us, length us, event | category | flops | bytes accessed | tf_op | source)
XLA Modules:
  0.0 61.0 jit_solution(13552906118355505253)
XLA Ops:
  0.7 58.3 %shard_map.46 = f32[32,128,256]{2,1,0:T(8,128)S(1)} custom-call(bf16[3,32,192,384]{3,2,1,0:T(8,128)(2,1)} %tiles.1, s32[2,3]{1,0:T(2,128)} %offsets_hbm.1, s32[3]{0:T(128)} %shifts_hbm.1, s32[1]{0:T(128)S(6)} %copy.7.counts_hbm), custom_call_target="tpu_custom_call" | custom-call | tf_op jit(solution)/shard_map/pallas_call | solution.py:426
  59.0 2.0 %copy.6 = f32[32,128,256]{2,1,0:T(8,128)} copy(f32[32,128,256]{2,1,0:T(8,128)S(1)} %shard_map.46) | data formatting | bytes 8388608

commit v3 on v2

--- a/solution.py
+++ b/solution.py
@@ -306,23 +306,37 @@
     def finish(i):
         z = NZ - 1 - i
 
-        @pl.when(has_low)
-        def _():
-            out[z, :, :RY] += from_low_mid[i]
-
-        @pl.when(has_high)
-        def _():
-            out[z, :, RY:] += from_high_mid[i]
-
-        @pl.when(has_left)
-        def _():
-            out[z, :RX] += from_left[i]
-
-        @pl.when(has_right)
-        def _():
-            out[z, RX:] += from_right[i]
-
-        out[z] *= inverse[...]
+        inner = has_low & has_high & has_left & has_right
+
+        @pl.when(inner)
+        def _():
+            for rows, flank in ((slice(0, RX), from_left), (slice(RX, BX), from_right)):
+                for lanes, halo in (
+                    (slice(0, RY), from_low_mid), (slice(RY, BY), from_high_mid)
+                ):
+                    out[z, rows, lanes] = (
+                        out[z, rows, lanes] + halo[i, rows] + flank[i, :, lanes]
+                    ) * inverse[rows, lanes]
+
+        @pl.when(jnp.logical_not(inner))
+        def _():
+            @pl.when(has_low)
+            def _():
+                out[z, :, :RY] += from_low_mid[i]
+
+            @pl.when(has_high)
+            def _():
+                out[z, :, RY:] += from_high_mid[i]
+
+            @pl.when(has_left)
+            def _():
+                out[z, :RX] += from_left[i]
+
+            @pl.when(has_right)
+            def _():
+                out[z, RX:] += from_right[i]
+
+            out[z] *= inverse[...]
 
     def alone(i):
         return (i < EDGE) | (i >= NZ - EDGE)
@@ -341,8 +355,8 @@
                 load_lot((i + 1 - EDGE) // LOT).wait()
 
             along_z(now, then)
+            along_x(i, True)
             along_y(jnp.maximum(z, 0), then)
-            along_x(i, True)
             along_x(i, False)
             start(y_ways, rim, i, 1)
 

time: 61.1 us -> 61.1 us (level)
  no operation moved by 1% of the time
where the time goes in v3:
time: 61.1 us; the launch traced here: 60.9 us
  Pallas kernels  58.3 us (95%)
  local copies, waits for them, and re-layouts  2.02 us (3%)
  between operations  0.66 us (1%)
    pallas_call x1, Pallas kernels, local(): pl.pallas_call(kernel, out_shape=pltpu.VMEM((NZ, BX, BY), jnp.float32), i...  58.3 us
    unnamed x1, local copies, waits for them, and re-layouts  2.02 us

profile of v3, /device:TPU:15, one launch (start us, length us, event | category | flops | bytes accessed | tf_op | source)
XLA Modules:
  0.0 60.9 jit_solution(7077748147280640839)
XLA Ops:
  0.7 58.3 %shard_map.46 = f32[32,128,256]{2,1,0:T(8,128)S(1)} custom-call(bf16[3,32,192,384]{3,2,1,0:T(8,128)(2,1)} %tiles.1, s32[2,3]{1,0:T(2,128)} %offsets_hbm.1, s32[3]{0:T(128)} %shifts_hbm.1, s32[1]{0:T(128)S(6)} %copy.7.counts_hbm), custom_call_target="tpu_custom_call" | custom-call | tf_op jit(solution)/shard_map/pallas_call | solution.py:440
  58.9 2.0 %copy.6 = f32[32,128,256]{2,1,0:T(8,128)} copy(f32[32,128,256]{2,1,0:T(8,128)S(1)} %shard_map.46) | data formatting | bytes 8388608
